TPU v7x, 16 devices: a 4x2x1 block of a 4x4x8 slice. The times are simulated.
16 devices in a mesh: prob: 2 (over y, z), feat: 8 (over x, core).
Axes of the slice: x: 4, y: 2, z: 1, core: 2. Of those that a mesh axis runs over, the one named last changes fastest.
The devices are a block of a 4x4x8 slice.
Arguments:
- x_data: bfloat16 [8192, 784], P('prob'), parts along dimension 0
- targets: float32 [8192], P('prob'), parts along dimension 0
- w_in: float32 [1024, 784], P(('prob', 'feat')), parts along dimension 0
- w_out: float32 [1024], P(('prob', 'feat')), parts along dimension 0
- reg_weight: float32 [2], P('prob'), parts along dimension 0
- step_size: float32 [2], P('prob'), parts along dimension 0
Outputs:
- output 1: float32 [1024, 784], P(('prob', 'feat')), parts along dimension 0
- output 2: float32 [1024], P(('prob', 'feat')), parts along dimension 0
- output 3: float32 [12], P('prob'), parts along dimension 0
There are 2 independent parts. A program takes and returns all parts, laid end to end along the dimension named above; each array names one.
All inputs are finite; a program needn't handle non-finite values.
Results may differ from a plain program's by a relative error of at most 0.001.
Values are sent between devices in bfloat16 or wider.
A program may use at most 768 MiB of HBM per device.

v0:
```python
import math
import jax
import jax.numpy as jnp
from jax import lax
from jax.sharding import PartitionSpec as P

NUM_ITERS = 6
HIST_LEN = 3
FULL_PREC = lax.Precision.HIGHEST


def pair_dot_local(first, second):
    return jnp.sum(first[0] * second[0]) + jnp.sum(first[1] * second[1])


def pair_axpy(base, coef, other):
    return (base[0] + coef * other[0], base[1] + coef * other[1])


def two_loop(full_grad, hist_s, hist_y, rho_vals, gamma_scale, dot_fn):
    query_vec = full_grad
    a_coefs = {}
    for pos_idx in reversed(range(len(hist_s))):
        a_coefs[pos_idx] = rho_vals[pos_idx] * dot_fn(hist_s[pos_idx], query_vec)
        query_vec = pair_axpy(query_vec, -a_coefs[pos_idx], hist_y[pos_idx])
    result = (gamma_scale * query_vec[0], gamma_scale * query_vec[1])
    for pos_idx in range(len(hist_s)):
        b_coef = rho_vals[pos_idx] * dot_fn(hist_y[pos_idx], result)
        result = pair_axpy(result, a_coefs[pos_idx] - b_coef, hist_s[pos_idx])
    return result


def global_dot(first, second):
    return lax.psum(pair_dot_local(first, second), "feat")


def solution(mesh):
    feat_size = mesh.shape["feat"]

    def local_solve(x_loc, t_loc, win_loc, wout_loc, reg_loc, step_loc):
        num_rows = x_loc.shape[0]
        in_scale = 1.0 / math.sqrt(x_loc.shape[1])
        out_scale = 1.0 / math.sqrt(win_loc.shape[0] * feat_size)
        reg_coef = reg_loc[0]
        step_coef = step_loc[0]
        x_f32 = x_loc.astype(jnp.float32)
        params = (win_loc, wout_loc)
        prev_params = params
        prev_grad = params
        hist_s = []
        hist_y = []
        rho_vals = []
        losses = []
        for iter_idx in range(NUM_ITERS):
            pre_act = lax.dot_general(x_f32, params[0], (((1,), (1,)), ((), ())), precision=FULL_PREC) * in_scale
            hid_act = jnp.tanh(pre_act)
            part_logits = jnp.dot(hid_act, params[1], precision=FULL_PREC) * out_scale
            logits = lax.psum(part_logits, "feat")
            losses.append(jnp.mean(jax.nn.softplus(logits) - t_loc * logits))
            resid_vec = (jax.nn.sigmoid(logits) - t_loc) / num_rows
            grad_out = jnp.dot(resid_vec, hid_act, precision=FULL_PREC) * out_scale
            d_pre = resid_vec[:, None] * (params[1] * (out_scale * in_scale))[None, :] * (1.0 - hid_act * hid_act)
            grad_in = lax.dot_general(d_pre, x_f32, (((0,), (0,)), ((), ())), precision=FULL_PREC)
            full_grad = (grad_in + reg_coef * params[0], grad_out + reg_coef * params[1])
            if iter_idx == 0:
                direction = full_grad
            else:
                s_vec = pair_axpy(params, -1.0, prev_params)
                y_vec = pair_axpy(full_grad, -1.0, prev_grad)
                curv_pair = lax.psum(jnp.stack([pair_dot_local(y_vec, s_vec), pair_dot_local(y_vec, y_vec)]), "feat")
                hist_s = (hist_s + [s_vec])[-HIST_LEN:]
                hist_y = (hist_y + [y_vec])[-HIST_LEN:]
                rho_vals = (rho_vals + [1.0 / curv_pair[0]])[-HIST_LEN:]
                gamma_scale = curv_pair[0] / curv_pair[1]
                direction = two_loop(full_grad, hist_s, hist_y, rho_vals, gamma_scale, global_dot)
            prev_params = params
            prev_grad = full_grad
            params = pair_axpy(params, -step_coef, direction)
        return params[0], params[1], jnp.stack(losses)

    specs_in = (P("prob", None), P("prob"), P(("prob", "feat"), None), P(("prob", "feat")), P("prob"), P("prob"))
    specs_out = (P(("prob", "feat"), None), P(("prob", "feat")), P("prob"))
    return jax.shard_map(local_solve, mesh=mesh, in_specs=specs_in, out_specs=specs_out, check_vma=False)
```

profile of v0, /device:TPU:113, one launch (start us, length us, event | category | flops | bytes accessed | tf_op | source)
XLA Modules:
  0.0 667.0 jit_solution(693080978889817326)
XLA Ops:
  9.4 24.0 %psum.245 = f32[4096]{0:T(1024)S(1)} all-reduce(f32[4096]{0:T(1024)S(1)} %broadcast_multiply_fusion.5), channel_id=1, replica_groups=mesh['prob'=2,'feat'=8] {'feat'}, use_global_device_ids=true, to_apply=%region_0.0 | all-reduce | flops 4096 | bytes 32768 | tf_op jit(solution)/shard_map/psum | solution.py:58
  49.3 23.6 %psum.246 = f32[4096]{0:T(1024)S(1)} all-reduce(f32[4096]{0:T(1024)S(1)} %broadcast_multiply_fusion.4), channel_id=1, replica_groups=mesh['prob'=2,'feat'=8] {'feat'}, use_global_device_ids=true, to_apply=%region_1.2 | all-reduce | flops 4096 | bytes 32768 | tf_op jit(solution)/shard_map/psum | solution.py:58
  73.0 9.0 %multiply_reduce_fusion.31 = (f32[]{:T(128)}, f32[]{:T(128)}, f32[]{:T(128)}, f32[64,784]{1,0:T(8,128)S(1)}, f32[64,784]{1,0:T(8,128)S(1)}, /*index=5*/f32[64,784]{1,0:T(8,128)S(1)}) fusion(f32[64,784]{1,0:T(8,128)S(1)} %get-tuple-element.123, f32[64,784]{1,0:T(8,128)S(1)} %get-tuple-element.122, f32[64,784]{1,0:T(8,128)S(1)} %copy-done, f32[]{:T(128)} %bitcast.146, ...), kind=kOutput, calls=%fused_computation.146 | convolution fusion | flops 2467901440 | bytes 8691984 | tf_op jit(solution)/shard_map/dot_general | solution.py:63
  87.5 15.9 %all-reduce.4 = (f32[2]{0:T(128)S(1)}, f32[]{:T(128)}) all-reduce(f32[2]{0:T(128)S(1)} %pad_maximum_fusion, f32[]{:T(128)S(6)} %add.499), channel_id=1, replica_groups=mesh['prob'=2,'feat'=8] {'feat'}, use_global_device_ids=true, to_apply=%region_6.7 | all-reduce | flops 3 | bytes 24 | tf_op jit(solution)/shard_map/psum | solution.py:70
  109.1 13.3 %psum.249 = f32[]{:T(128)} all-reduce(f32[]{:T(128)S(6)} %add.502), channel_id=1, replica_groups=mesh['prob'=2,'feat'=8] {'feat'}, use_global_device_ids=true, to_apply=%region_12.13 | all-reduce | flops 1 | bytes 8 | tf_op jit(solution)/shard_map/psum | solution.py:34
  129.8 20.8 %psum.250 = f32[4096]{0:T(1024)S(1)} all-reduce(f32[4096]{0:T(1024)S(1)} %broadcast_multiply_fusion.3), channel_id=1, replica_groups=mesh['prob'=2,'feat'=8] {'feat'}, use_global_device_ids=true, to_apply=%region_13.14 | all-reduce | flops 4096 | bytes 32768 | tf_op jit(solution)/shard_map/psum | solution.py:58
  165.0 15.9 %all-reduce.3 = (f32[2]{0:T(128)S(1)}, f32[]{:T(128)}) all-reduce(f32[2]{0:T(128)S(1)} %pad_maximum_fusion.1, f32[]{:T(128)S(6)} %add.516), channel_id=1, replica_groups=mesh['prob'=2,'feat'=8] {'feat'}, use_global_device_ids=true, to_apply=%region_18.19 | all-reduce | flops 3 | bytes 24 | tf_op jit(solution)/shard_map/psum | solution.py:70
  185.3 13.0 %psum.253 = f32[]{:T(128)} all-reduce(f32[]{:T(128)S(6)} %add.519), channel_id=1, replica_groups=mesh['prob'=2,'feat'=8] {'feat'}, use_global_device_ids=true, to_apply=%region_24.25 | all-reduce | flops 1 | bytes 8 | tf_op jit(solution)/shard_map/psum | solution.py:34
  202.7 13.0 %psum.254 = f32[]{:T(128)} all-reduce(f32[]{:T(128)S(6)} %add.522), channel_id=1, replica_groups=mesh['prob'=2,'feat'=8] {'feat'}, use_global_device_ids=true, to_apply=%region_27.28 | all-reduce | flops 1 | bytes 8 | tf_op jit(solution)/shard_map/psum | solution.py:34
  218.8 13.0 %psum.255 = f32[]{:T(128)} all-reduce(f32[]{:T(128)S(6)} %add.525), channel_id=1, replica_groups=mesh['prob'=2,'feat'=8] {'feat'}, use_global_device_ids=true, to_apply=%region_30.31 | all-reduce | flops 1 | bytes 8 | tf_op jit(solution)/shard_map/psum | solution.py:34
  239.1 21.0 %psum.256 = f32[4096]{0:T(1024)S(1)} all-reduce(f32[4096]{0:T(1024)S(1)} %broadcast_multiply_fusion.2), channel_id=1, replica_groups=mesh['prob'=2,'feat'=8] {'feat'}, use_global_device_ids=true, to_apply=%region_31.32 | all-reduce | flops 4096 | bytes 32768 | tf_op jit(solution)/shard_map/psum | solution.py:58
  274.6 15.9 %all-reduce.2 = (f32[2]{0:T(128)S(1)}, f32[]{:T(128)}) all-reduce(f32[2]{0:T(128)S(1)} %pad_maximum_fusion.2, f32[]{:T(128)S(6)} %add.539), channel_id=1, replica_groups=mesh['prob'=2,'feat'=8] {'feat'}, use_global_device_ids=true, to_apply=%region_36.37 | all-reduce | flops 3 | bytes 24 | tf_op jit(solution)/shard_map/psum | solution.py:70
  295.0 13.0 %psum.259 = f32[]{:T(128)} all-reduce(f32[]{:T(128)S(6)} %add.542), channel_id=1, replica_groups=mesh['prob'=2,'feat'=8] {'feat'}, use_global_device_ids=true, to_apply=%region_42.43 | all-reduce | flops 1 | bytes 8 | tf_op jit(solution)/shard_map/psum | solution.py:34
  311.2 13.0 %psum.260 = f32[]{:T(128)} all-reduce(f32[]{:T(128)S(6)} %add.545), channel_id=1, replica_groups=mesh['prob'=2,'feat'=8] {'feat'}, use_global_device_ids=true, to_apply=%region_45.46 | all-reduce | flops 1 | bytes 8 | tf_op jit(solution)/shard_map/psum | solution.py:34
  328.7 13.1 %psum.261 = f32[]{:T(128)} all-reduce(f32[]{:T(128)S(6)} %add.548), channel_id=1, replica_groups=mesh['prob'=2,'feat'=8] {'feat'}, use_global_device_ids=true, to_apply=%region_48.49 | all-reduce | flops 1 | bytes 8 | tf_op jit(solution)/shard_map/psum | solution.py:34
  345.0 13.0 %psum.262 = f32[]{:T(128)} all-reduce(f32[]{:T(128)S(6)} %add.551), channel_id=1, replica_groups=mesh['prob'=2,'feat'=8] {'feat'}, use_global_device_ids=true, to_apply=%region_51.52 | all-reduce | flops 1 | bytes 8 | tf_op jit(solution)/shard_map/psum | solution.py:34
  361.2 13.0 %psum.263 = f32[]{:T(128)} all-reduce(f32[]{:T(128)S(6)} %add.554), channel_id=1, replica_groups=mesh['prob'=2,'feat'=8] {'feat'}, use_global_device_ids=true, to_apply=%region_54.55 | all-reduce | flops 1 | bytes 8 | tf_op jit(solution)/shard_map/psum | solution.py:34
  381.6 20.8 %psum.264 = f32[4096]{0:T(1024)S(1)} all-reduce(f32[4096]{0:T(1024)S(1)} %broadcast_multiply_fusion.1), channel_id=1, replica_groups=mesh['prob'=2,'feat'=8] {'feat'}, use_global_device_ids=true, to_apply=%region_55.56 | all-reduce | flops 4096 | bytes 32768 | tf_op jit(solution)/shard_map/psum | solution.py:58
  402.4 9.0 %multiply_reduce_fusion.13 = (f32[]{:T(128)}, f32[]{:T(128)}, f32[]{:T(128)}, f32[64,784]{1,0:T(8,128)S(1)}, f32[64,784]{1,0:T(8,128)S(1)}, /*index=5*/f32[64,784]{1,0:T(8,128)S(1)}) fusion(f32[64,784]{1,0:T(8,128)S(1)} %get-tuple-element.128, f32[64,784]{1,0:T(8,128)S(1)} %multiply_add_fusion.14, f32[64,784]{1,0:T(8,128)S(1)} %multiply_add_fusion.21, ...), kind=kOutput, calls=%fused_computation.110 | convolution fusion | flops 2467901440 | bytes 8691984 | tf_op jit(solution)/shard_map/dot_general | solution.py:63
  416.9 15.9 %all-reduce.1 = (f32[2]{0:T(128)S(1)}, f32[]{:T(128)}) all-reduce(f32[2]{0:T(128)S(1)} %pad_maximum_fusion.3, f32[]{:T(128)S(6)} %add.568), channel_id=1, replica_groups=mesh['prob'=2,'feat'=8] {'feat'}, use_global_device_ids=true, to_apply=%region_60.61 | all-reduce | flops 3 | bytes 24 | tf_op jit(solution)/shard_map/psum | solution.py:70
  437.3 13.0 %psum.267 = f32[]{:T(128)} all-reduce(f32[]{:T(128)S(6)} %add.571), channel_id=1, replica_groups=mesh['prob'=2,'feat'=8] {'feat'}, use_global_device_ids=true, to_apply=%region_66.67 | all-reduce | flops 1 | bytes 8 | tf_op jit(solution)/shard_map/psum | solution.py:34
  453.5 13.0 %psum.268 = f32[]{:T(128)} all-reduce(f32[]{:T(128)S(6)} %add.574), channel_id=1, replica_groups=mesh['prob'=2,'feat'=8] {'feat'}, use_global_device_ids=true, to_apply=%region_69.70 | all-reduce | flops 1 | bytes 8 | tf_op jit(solution)/shard_map/psum | solution.py:34
  471.1 13.1 %psum.269 = f32[]{:T(128)} all-reduce(f32[]{:T(128)S(6)} %add.577), channel_id=1, replica_groups=mesh['prob'=2,'feat'=8] {'feat'}, use_global_device_ids=true, to_apply=%region_72.73 | all-reduce | flops 1 | bytes 8 | tf_op jit(solution)/shard_map/psum | solution.py:34
  487.5 13.3 %psum.270 = f32[]{:T(128)} all-reduce(f32[]{:T(128)S(6)} %add.580), channel_id=1, replica_groups=mesh['prob'=2,'feat'=8] {'feat'}, use_global_device_ids=true, to_apply=%region_75.76 | all-reduce | flops 1 | bytes 8 | tf_op jit(solution)/shard_map/psum | solution.py:34
  504.1 13.0 %psum.271 = f32[]{:T(128)} all-reduce(f32[]{:T(128)S(6)} %add.583), channel_id=1, replica_groups=mesh['prob'=2,'feat'=8] {'feat'}, use_global_device_ids=true, to_apply=%region_78.79 | all-reduce | flops 1 | bytes 8 | tf_op jit(solution)/shard_map/psum | solution.py:34
  524.5 20.8 %psum.272 = f32[4096]{0:T(1024)S(1)} all-reduce(f32[4096]{0:T(1024)S(1)} %broadcast_multiply_fusion), channel_id=1, replica_groups=mesh['prob'=2,'feat'=8] {'feat'}, use_global_device_ids=true, to_apply=%region_79.80 | all-reduce | flops 4096 | bytes 32768 | tf_op jit(solution)/shard_map/psum | solution.py:58
  560.4 15.9 %all-reduce = (f32[2]{0:T(128)S(1)}, f32[]{:T(128)}) all-reduce(f32[2]{0:T(128)S(1)} %pad_maximum_fusion.4, f32[]{:T(128)S(6)} %add.597), channel_id=1, replica_groups=mesh['prob'=2,'feat'=8] {'feat'}, use_global_device_ids=true, to_apply=%region_84.85 | all-reduce | flops 3 | bytes 24 | tf_op jit(solution)/shard_map/psum | solution.py:70
  580.8 13.0 %psum.275 = f32[]{:T(128)} all-reduce(f32[]{:T(128)S(6)} %add.600), channel_id=1, replica_groups=mesh['prob'=2,'feat'=8] {'feat'}, use_global_device_ids=true, to_apply=%region_90.91 | all-reduce | flops 1 | bytes 8 | tf_op jit(solution)/shard_map/psum | solution.py:34
  597.1 13.0 %psum.276 = f32[]{:T(128)} all-reduce(f32[]{:T(128)S(6)} %add.603), channel_id=1, replica_groups=mesh['prob'=2,'feat'=8] {'feat'}, use_global_device_ids=true, to_apply=%region_93.94 | all-reduce | flops 1 | bytes 8 | tf_op jit(solution)/shard_map/psum | solution.py:34
  614.8 13.0 %psum.277 = f32[]{:T(128)} all-reduce(f32[]{:T(128)S(6)} %add.606), channel_id=1, replica_groups=mesh['prob'=2,'feat'=8] {'feat'}, use_global_device_ids=true, to_apply=%region_96.97 | all-reduce | flops 1 | bytes 8 | tf_op jit(solution)/shard_map/psum | solution.py:34
  631.0 13.0 %psum.278 = f32[]{:T(128)} all-reduce(f32[]{:T(128)S(6)} %add.609), channel_id=1, replica_groups=mesh['prob'=2,'feat'=8] {'feat'}, use_global_device_ids=true, to_apply=%region_99.100 | all-reduce | flops 1 | bytes 8 | tf_op jit(solution)/shard_map/psum | solution.py:34
  647.2 13.0 %psum.279 = f32[]{:T(128)} all-reduce(f32[]{:T(128)S(6)} %add.612), channel_id=1, replica_groups=mesh['prob'=2,'feat'=8] {'feat'}, use_global_device_ids=true, to_apply=%region_102.103 | all-reduce | flops 1 | bytes 8 | tf_op jit(solution)/shard_map/psum | solution.py:34
  (99 shorter events, 116.1 us)
Async XLA Ops:
  1.3 7.4 %copy-start.2 = (f32[64]{0:T(128)S(1)}, f32[64]{0:T(128)}, u32[]{:S(2)}) copy-start(f32[64]{0:T(128)} %param.9) | copy-start | bytes 772
  1.9 31.5 %copy-start.1 = (f32[4096]{0:T(1024)S(1)}, f32[4096]{0:T(1024)}, u32[]{:S(2)}) copy-start(f32[4096]{0:T(1024)} %param.7) | copy-start | bytes 49156
  2.0 32.4 %copy-start = (f32[64,784]{1,0:T(8,128)S(1)}, f32[64,784]{1,0:T(8,128)}, u32[]{:S(2)}) copy-start(f32[64,784]{1,0:T(8,128)} %param.8) | copy-start | bytes 602116
where the time goes:
time: 677 us; the launch traced here: 667 us
  blocking collectives  458 us (68%)
  matrix products  103 us (15%)
  between operations  74.7 us (11%)
  other arithmetic  27.6 us (4%)
    psum x19, blocking collectives, global_dot(): return lax.psum(pair_dot_local(first, second), 'feat')  248 us
    psum x6, blocking collectives, local_solve(): logits = lax.psum(part_logits, 'feat')  131 us
    psum x5, blocking collectives, local_solve(): lax.psum(jnp.stack([pair_dot_local(y_vec, s_vec), pair_dot_local(y_vec, y...  79.4 us
    dot_general x6, matrix products, local_solve(): lax.dot_general(d_pre, x_f32, (((0,), (0,)), ((), ())), precision=FULL_PREC)  53.3 us
    dot_general x6, matrix products, local_solve(): lax.dot_general(x_f32, params[0], (((1,), (1,)), ((), ())), precision=FUL...  36.7 us
    reduce_sum x38, other arithmetic, pair_dot_local(): return jnp.sum(first[0] * second[0]) + jnp.sum(first[1] * second[1])  24.8 us

commit v1 on v0

v1 whole, which is shorter than its diff:
```python
import functools
import math

import jax
import jax.numpy as jnp
from jax import lax
from jax.experimental import pallas as pl
from jax.experimental.pallas import tpu as pltpu
from jax.sharding import PartitionSpec as P

NUM_ITERS = 6
HIST = 3
CHUNKS = 4
LANES = 128
F32 = jnp.float32
BF16 = jnp.bfloat16
MESH = pl.DeviceIdType.MESH


def split3(v):
    hi = v.astype(BF16)
    rest = v - hi.astype(F32)
    mid = rest.astype(BF16)
    lo = (rest - mid.astype(F32)).astype(BF16)
    return hi, mid, lo


def kernel(
    n, rows, hid, dim, out_units,
    x_hbm, t_ref, w_ref, wo_ref, reg_ref, step_ref,
    wnew_ref, wonew_ref, loss_ref,
    xv, xt, q_ref, h_ref, u_ref, d3_ref, g3_ref, acc_ref, theta, g_ref, s_ref, y_ref, w2b_ref,
    zbuf, r_ref, dbuf, row_ref, lacc,
    xsem, zsend, zrecv, dsend, drecv,
):
    main = dim // LANES * LANES
    tail = dim - main
    width = main + LANES
    tiles = width // LANES
    groups = hid // 8
    per = rows // CHUNKS
    blocks = per // LANES
    in_scale = 1.0 / math.sqrt(dim)
    out_scale = 1.0 / math.sqrt(out_units)
    me = lax.axis_index("feat")
    reg = reg_ref[0]
    step = step_ref[0]

    def peer(d):
        return lax.rem(me + d, n)

    order = sorted(range(1, n), key=lambda d: -min(d, n - d))

    copies = [
        pltpu.make_async_copy(x_hbm.at[pl.ds(c * per, per)], xv.at[pl.ds(c * per, per)], xsem.at[c])
        for c in range(CHUNKS)
    ]
    for copy in copies:
        copy.start()
    barrier = pltpu.get_barrier_semaphore()
    for d in order:
        pl.semaphore_signal(barrier, inc=1, device_id={"feat": peer(d)}, device_id_type=MESH)

    lane8 = lax.broadcasted_iota(jnp.int32, (8, LANES), 1)
    lane = lax.broadcasted_iota(jnp.int32, (hid, LANES), 1)
    sub = lax.broadcasted_iota(jnp.int32, (hid, LANES), 0)

    def g8(v):
        return v.reshape(groups, 8, LANES)

    def col(t):
        return pl.ds(t * LANES, LANES)

    w2row = wo_ref[...]
    w2col = jnp.sum(jnp.where(lane[:, :hid] == sub[:, :hid], w2row, 0.0), axis=1, keepdims=True)
    theta[:, main:width] = jnp.where(lane == tail, w2col, 0.0)
    theta[:, 0:main] = w_ref[:, 0:main]
    theta[:, main:dim] = w_ref[:, main:dim]
    w2b_ref[...] = jnp.broadcast_to(w2col, (hid, LANES))
    s_ref[...] = jnp.zeros_like(s_ref)
    y_ref[...] = jnp.zeros_like(y_ref)
    for j in range(1, NUM_ITERS):
        q_ref[j] = jnp.zeros((hid, rows), F32)

    def pieces(src):
        for t in range(tiles):
            v = src[:, col(t)]
            if t == tiles - 1:
                v = jnp.where(lane < tail, v, 0.0)
            for i, piece in enumerate(split3(v)):
                g3_ref[i * hid:(i + 1) * hid, col(t)] = piece

    def forward(slot, c):
        rs = pl.ds(c * per, per)
        prod = lax.dot_general(g3_ref[:, 0:main], xv[rs, 0:main], (((1,), (1,)), ((), ())), preferred_element_type=F32)
        prod += lax.dot_general(g3_ref[:, main:width], xt[rs, :], (((1,), (1,)), ((), ())), preferred_element_type=F32)
        q_ref[slot, :, rs] = prod[0:hid] + (prod[hid:2 * hid] + prod[2 * hid:3 * hid])

    pieces(theta)
    for c in range(CHUNKS):
        rs = pl.ds(c * per, per)
        copies[c].wait()
        xt[rs, :] = jnp.zeros((per, LANES), BF16)
        xt[rs, 0:tail] = xv[rs, main:dim]
        forward(0, c)

    def zcopy(par, c, d):
        return pltpu.make_async_remote_copy(
            src_ref=zbuf.at[par, c, me], dst_ref=zbuf.at[par, c, me],
            send_sem=zsend.at[c, d], recv_sem=zrecv.at[par, c, me],
            device_id={"feat": peer(d)}, device_id_type=MESH)

    def zarrive(par, c, d):
        source = peer(n - d)
        return pltpu.make_async_remote_copy(
            src_ref=zbuf.at[par, c, source], dst_ref=zbuf.at[par, c, source],
            send_sem=zsend.at[c, d], recv_sem=zrecv.at[par, c, source],
            device_id={"feat": source}, device_id_type=MESH)

    def dcopy(d):
        return pltpu.make_async_remote_copy(
            src_ref=dbuf.at[me], dst_ref=dbuf.at[me], send_sem=dsend.at[d], recv_sem=drecv.at[me],
            device_id={"feat": peer(d)}, device_id_type=MESH)

    def darrive(d):
        source = peer(n - d)
        return pltpu.make_async_remote_copy(
            src_ref=dbuf.at[source], dst_ref=dbuf.at[source], send_sem=dsend.at[d], recv_sem=drecv.at[source],
            device_id={"feat": source}, device_id_type=MESH)

    def logits(par, coefs):
        for c in range(CHUNKS):
            for b in range(blocks):
                cs = col(c * blocks + b)
                pre = coefs[0] * g8(q_ref[0, :, cs])
                for j in range(1, len(coefs)):
                    pre += coefs[j] * g8(q_ref[j, :, cs])
                act = jnp.tanh(pre)
                h_ref[:, cs] = act.reshape(hid, LANES)
                part = jnp.sum(act * g8(w2b_ref[...]), axis=0)
                zbuf[par, c, me, b:b + 1, :] = jnp.sum(part, axis=0, keepdims=True) * out_scale
            for d in order:
                zcopy(par, c, d).start()
        for b in range(rows // LANES):
            act = h_ref[:, col(b)]
            u_ref[:, col(b)] = w2b_ref[...] * (1.0 - act * act)

    def gradient(it, par):
        loss = jnp.zeros((8, LANES), F32)
        gw2 = jnp.zeros((groups, 8, LANES), F32)
        for c in range(CHUNKS):
            for d in order:
                zarrive(par, c, d).wait_recv()
            z = zbuf[par, c, 0]
            for i in range(1, n):
                z += zbuf[par, c, i]
            t = t_ref[c * blocks:(c + 1) * blocks, :]
            loss += jnp.maximum(z, 0.0) + jnp.log1p(jnp.exp(-jnp.abs(z))) - t * z
            r_ref[c * blocks:(c + 1) * blocks, :] = jax.nn.sigmoid(z) - t
            for b in range(blocks):
                i = c * blocks + b
                rrow = r_ref[i:i + 1, :]
                gw2 += g8(h_ref[:, col(i)] * rrow)
                for p, piece in enumerate(split3(u_ref[:, col(i)] * rrow)):
                    d3_ref[p * hid:(p + 1) * hid, col(i)] = piece
            rs = pl.ds(c * per, per)
            lhs = d3_ref[:, rs]
            pm = jnp.dot(lhs, xv[rs, 0:main], preferred_element_type=F32)
            pt = jnp.dot(lhs, xt[rs, :], preferred_element_type=F32)
            if c == 0:
                acc_ref[:, 0:main] = pm
                acc_ref[:, main:width] = pt
            else:
                acc_ref[:, 0:main] += pm
                acc_ref[:, main:width] += pt
        lacc[it] = loss
        gw2 = jnp.sum(gw2.reshape(hid, LANES), axis=1, keepdims=True)
        for t in range(tiles):
            total = acc_ref[0:hid, col(t)] + (acc_ref[hid:2 * hid, col(t)] + acc_ref[2 * hid:3 * hid, col(t)])
            total = total * (in_scale * out_scale / rows)
            if t == tiles - 1:
                total = jnp.where(lane == tail, gw2 * (out_scale / rows), total)
            g_ref[:, col(t)] = total + reg * theta[:, col(t)]
        for c in range(CHUNKS):
            for d in order:
                zcopy(par, c, d).wait_send()

    def coefs_of(e, count):
        e = e * in_scale
        return [jnp.broadcast_to(e[:, j:j + 1], (8, LANES)) for j in range(count)]

    def broadcast(v):
        return jnp.broadcast_to(v, (8, LANES))

    pl.semaphore_wait(barrier, n - 1)
    zero = jnp.zeros((8, LANES), F32)

    logits(0, coefs_of(jnp.where(lane8 == 0, 1.0, zero), 1))
    gradient(0, 0)
    pieces(g_ref)
    for c in range(CHUNKS):
        forward(1, c)
    for t in range(tiles):
        s = -step * g_ref[:, col(t)]
        s_ref[0, :, col(t)] = s
        theta[:, col(t)] += s
    sig = jnp.where(lane8 == 1, -step, zero)
    e = jnp.where(lane8 == 0, 1.0, sig)

    for i in range(6):
        row_ref[i] = zero
    for i, v in enumerate((sig, zero, zero, e)):
        row_ref[6 + i] = v

    def body(k, carry):
        rho1, rho2, sy21, yy11, yy12, yy22, sig0, sig1, sig2, e = (row_ref[i] for i in range(10))
        par = lax.rem(k, 2)
        slots = [lax.rem(k + 2 - a, HIST) for a in range(HIST)]
        last = width - LANES
        w2b_ref[...] = jnp.broadcast_to(theta[:, last + tail:last + tail + 1], (hid, LANES))
        logits(par, coefs_of(e, NUM_ITERS))
        for t in range(tiles):
            y_ref[slots[0], :, col(t)] = g_ref[:, col(t)]
        gradient(k, par)
        dots = [jnp.zeros((8, LANES), F32)] * 12
        for t in range(tiles):
            g = g8(g_ref[:, col(t)])
            y0 = g - g8(y_ref[slots[0], :, col(t)])
            y_ref[slots[0], :, col(t)] = y0.reshape(hid, LANES)
            ss = [g8(s_ref[slots[a], :, col(t)]) for a in range(HIST)]
            ys = [y0] + [g8(y_ref[slots[a], :, col(t)]) for a in range(1, HIST)]
            pairs = [(v, g) for v in ss] + [(v, g) for v in ys] + [(v, y0) for v in ss] + [(v, y0) for v in ys]
            dots = [d + jnp.sum(a * b, axis=0) for d, (a, b) in zip(dots, pairs)]
        row = jnp.zeros((1, LANES), F32)
        for i, d in enumerate(dots):
            d = jnp.sum(jnp.sum(d, axis=0, keepdims=True), axis=1, keepdims=True)
            row = jnp.where(lane8[0:1] == i, d, row)
        dbuf[me] = row
        for d in order:
            dcopy(d).start()

        @pl.when(k < NUM_ITERS - 1)
        def _():
            pieces(g_ref)
            for c in range(CHUNKS):
                forward(k + 1, c)

        for d in order:
            darrive(d).wait_recv()
        total = dbuf[0]
        for i in range(1, n):
            total += dbuf[i]
        vals = [broadcast(total[:, i:i + 1]) for i in range(12)]
        sg, yg, y0s, y0y = vals[0:3], vals[3:6], vals[6:9], vals[9:12]
        rho = [1.0 / y0s[0], rho1, rho2]
        gamma = y0s[0] / y0y[0]
        sy = {(1, 0): y0s[1], (2, 0): y0s[2], (2, 1): sy21}
        yy = {(0, 0): y0y[0], (0, 1): y0y[1], (0, 2): y0y[2], (1, 1): yy11, (1, 2): yy12, (2, 2): yy22}
        a = []
        for i in range(HIST):
            v = sg[i]
            for j in range(i):
                v = v - a[j] * sy[i, j]
            a.append(rho[i] * v)
        diff = [None] * HIST
        for i in reversed(range(HIST)):
            v = yg[i]
            for j in range(HIST):
                v = v - a[j] * yy[min(i, j), max(i, j)]
            v = gamma * v
            for j in range(i + 1, HIST):
                v = v + diff[j] * sy[j, i]
            diff[i] = a[i] - rho[i] * v
        cg = -step * gamma
        cy = [-cg * v for v in a]
        cs = [-step * v for v in diff]
        sigs = [sig0, sig1, sig2]
        new = jnp.where(lane8 == k + 1, cg, zero)
        for i in range(HIST):
            new = new + jnp.where(lane8 == k + 1 - i, cy[i], zero) - jnp.where(lane8 == k - i, cy[i], zero)
            new = new + cs[i] * sigs[i]
        for t in range(tiles):
            s = cg * g8(g_ref[:, col(t)])
            for i in range(HIST):
                s = s + cy[i] * g8(y_ref[slots[i], :, col(t)])
                s = s + cs[i] * g8(s_ref[slots[i], :, col(t)])
            s = s.reshape(hid, LANES)
            s_ref[slots[2], :, col(t)] = s
            theta[:, col(t)] += s
        for d in order:
            dcopy(d).wait_send()
        for i, v in enumerate((rho[0], rho[1], sy[1, 0], yy[0, 0], yy[0, 1], yy[1, 1], new, sig0, sig1, e + new)):
            row_ref[i] = v
        return carry

    lax.fori_loop(1, NUM_ITERS, body, 0)

    wnew_ref[:, 0:main] = theta[:, 0:main]
    wnew_ref[:, main:dim] = theta[:, main:dim]
    w2col = theta[:, dim:dim + 1]
    wonew_ref[...] = jnp.sum(jnp.where(lane == sub, w2col, 0.0), axis=0, keepdims=True)[:, 0:hid]
    for k in range(NUM_ITERS):
        loss_ref[k] = jnp.sum(lacc[k]) / rows


def solution(mesh):
    n = mesh.shape["feat"]

    def local_solve(x, t, w, wo, reg, step):
        rows, dim = x.shape
        hid = w.shape[0]
        width = dim // LANES * LANES + LANES
        per = rows // CHUNKS
        vmem = pl.BlockSpec(memory_space=pltpu.VMEM)
        smem = pl.BlockSpec(memory_space=pltpu.SMEM)
        wnew, wonew, losses = pl.pallas_call(
            functools.partial(kernel, n, rows, hid, dim, hid * n),
            out_shape=(
                jax.ShapeDtypeStruct((hid, dim), F32),
                jax.ShapeDtypeStruct((1, hid), F32),
                jax.ShapeDtypeStruct((NUM_ITERS,), F32),
            ),
            in_specs=[pl.BlockSpec(memory_space=pltpu.HBM), vmem, vmem, vmem, smem, smem],
            out_specs=(vmem, vmem, smem),
            scratch_shapes=[
                pltpu.VMEM((rows, dim), BF16),
                pltpu.VMEM((rows, LANES), BF16),
                pltpu.VMEM((NUM_ITERS, hid, rows), F32),
                pltpu.VMEM((hid, rows), F32),
                pltpu.VMEM((hid, rows), F32),
                pltpu.VMEM((3 * hid, rows), BF16),
                pltpu.VMEM((3 * hid, width), BF16),
                pltpu.VMEM((3 * hid, width), F32),
                pltpu.VMEM((hid, width), F32),
                pltpu.VMEM((hid, width), F32),
                pltpu.VMEM((HIST, hid, width), F32),
                pltpu.VMEM((HIST, hid, width), F32),
                pltpu.VMEM((hid, LANES), F32),
                pltpu.VMEM((2, CHUNKS, n, per // LANES, LANES), F32),
                pltpu.VMEM((rows // LANES, LANES), F32),
                pltpu.VMEM((n, 1, LANES), F32),
                pltpu.VMEM((10, 8, LANES), F32),
                pltpu.VMEM((NUM_ITERS, 8, LANES), F32),
                pltpu.SemaphoreType.DMA((CHUNKS,)),
                pltpu.SemaphoreType.DMA((CHUNKS, n)),
                pltpu.SemaphoreType.DMA((2, CHUNKS, n)),
                pltpu.SemaphoreType.DMA((n,)),
                pltpu.SemaphoreType.DMA((n,)),
            ],
            compiler_params=pltpu.CompilerParams(
                collective_id=0, has_side_effects=True, vmem_limit_bytes=56 * 1024 * 1024
            ),
        )(x, t.reshape(rows // LANES, LANES), w, wo.reshape(1, hid), reg, step)
        return wnew, wonew.reshape(hid), losses

    specs_in = (P("prob", None), P("prob"), P(("prob", "feat"), None), P(("prob", "feat")), P("prob"), P("prob"))
    specs_out = (P(("prob", "feat"), None), P(("prob", "feat")), P("prob"))
    return jax.shard_map(local_solve, mesh=mesh, in_specs=specs_in, out_specs=specs_out, check_vma=False)
```

time: 677 us -> 84.5 us (0.12); the launches traced: 667 us -> 84.1 us
  blocking collectives: 458 us -> 0 us
  matrix products: 103 us -> 0 us
  between operations: 74.7 us -> 1.93 us
  Pallas kernels: 0 us -> 67.9 us
  other arithmetic: 27.6 us -> 0 us
  local copies, waits for them, and re-layouts: 3.73 us -> 14.3 us
    psum x30 -> x0, blocking collectives: 458 us -> none  [the longest x19 248 us: global_dot(): return lax.psum(pair_dot_local(first, second), 'feat')]
    dot_general x24 -> x0, matrix products: 103 us -> none  [the longest x6 53.3 us: local_solve(): lax.dot_general(d_pre, x_f32, (((0,), (0,)), ((), ())), precision=FULL_PREC)]
    pallas_call x0 -> x1, Pallas kernels: none -> 67.9 us  [local_solve(): pl.pallas_call(functools.partial(kernel, n, rows, hid, dim, hid * n), out...]
    reduce_sum x39 -> x0, other arithmetic: 25.6 us -> none  [the longest x38 24.8 us: pair_dot_local(): return jnp.sum(first[0] * second[0]) + jnp.sum(first[1] * second[1])]
    unnamed x6 -> x4, local copies, waits for them, and re-layouts: 0.01 us -> 14.3 us
where the time goes in v1:
time: 84.5 us; the launch traced here: 84.1 us
  Pallas kernels  67.9 us (80%)
  local copies, waits for them, and re-layouts  14.3 us (17%)
  between operations  1.93 us (2%)
    pallas_call x1, Pallas kernels, local_solve(): pl.pallas_call(functools.partial(kernel, n, rows, hid, dim, hid * n), out...  67.9 us
    unnamed x4, local copies, waits for them, and re-layouts  14.3 us

profile of v1, /device:TPU:113, one launch (start us, length us, event | category | flops | bytes accessed | tf_op | source)
XLA Modules:
  0.0 84.1 jit_solution(9415267020876951818)
XLA Ops:
  1.9 10.4 %copy.9.x_hbm = bf16[4096,784]{1,0:T(8,128)(2,1)} copy(bf16[4096,784]{0,1:T(8,128)(2,1)} %param.6) | data formatting | bytes 12845056 | tf_op args[0]
  12.4 67.9 %shard_map.85 = (f32[64,784]{1,0:T(8,128)}, f32[1,64]{1,0:T(1,128)}, f32[6]{0:T(128)}) custom-call(bf16[4096,784]{1,0:T(8,128)(2,1)} %copy.9.x_hbm, f32[32,128]{1,0:T(8,128)} %bitcast.3, f32[64,784]{1,0:T(8,128)} %w_ref.1, f32[1,64]{1,0:T(1,128)} %bitcast.4, f32[1]{0:T(128)S(6)} %copy.13.reg_ref, f32[1]{0:T(128)S(6)} %copy.14.step_ref), custom_call_target="tpu_custom_call" | custom-call | tf_op jit(solution)/shard_map/pallas_call | solution.py:316
  80.2 1.6 %copy.15 = f32[64,784]{1,0:T(8,128)} copy(f32[64,784]{1,0:T(8,128)} %get-tuple-element.12) | data formatting | bytes 401408
  81.9 1.1 %copy.16 = f32[64]{0:T(128)} copy(f32[64]{0:T(128)} %bitcast.5) | data formatting | bytes 512
  83.0 1.2 %copy.17 = f32[6]{0:T(128)} copy(f32[6]{0:T(128)} %get-tuple-element.14) | data formatting | bytes 48

commit v2 on v1

--- a/solution.py
+++ b/solution.py
@@ -27,11 +27,11 @@
 
 def kernel(
     n, rows, hid, dim, out_units,
-    x_hbm, t_ref, w_ref, wo_ref, reg_ref, step_ref,
-    wnew_ref, wonew_ref, loss_ref,
-    xv, xt, q_ref, h_ref, u_ref, d3_ref, g3_ref, acc_ref, theta, g_ref, s_ref, y_ref, w2b_ref,
-    zbuf, r_ref, dbuf, row_ref, lacc,
-    xsem, zsend, zrecv, dsend, drecv,
+    x_hbm, t_hbm, w_hbm, wo_hbm, reg_hbm, step_hbm,
+    theta, lacc,
+    xv, xr, xt, t_ref, w_ref, wo_ref, reg_ref, step_ref, q_ref, h_ref, u_ref, d3_ref, g3_ref, gt_ref, acc_ref, g_ref, s_ref, y_ref, w2b_ref,
+    zbuf, r_ref, dbuf, row_ref,
+    xsem, isem, zsend, zrecv, dsend, drecv,
 ):
     main = dim // LANES * LANES
     tail = dim - main
@@ -43,8 +43,6 @@
     in_scale = 1.0 / math.sqrt(dim)
     out_scale = 1.0 / math.sqrt(out_units)
     me = lax.axis_index("feat")
-    reg = reg_ref[0]
-    step = step_ref[0]
 
     def peer(d):
         return lax.rem(me + d, n)
@@ -52,10 +50,15 @@
     order = sorted(range(1, n), key=lambda d: -min(d, n - d))
 
     copies = [
-        pltpu.make_async_copy(x_hbm.at[pl.ds(c * per, per)], xv.at[pl.ds(c * per, per)], xsem.at[c])
+        pltpu.make_async_copy(x_hbm.at[:, pl.ds(c * per, per)], xr.at[:, pl.ds(c * per, per)], xsem.at[c])
         for c in range(CHUNKS)
     ]
-    for copy in copies:
+    inputs = [
+        pltpu.make_async_copy(src, dst, isem.at[i])
+        for i, (src, dst) in enumerate(
+            ((w_hbm, w_ref), (wo_hbm, wo_ref), (t_hbm, t_ref), (reg_hbm, reg_ref), (step_hbm, step_ref)))
+    ]
+    for copy in inputs[:2] + copies + inputs[2:]:
         copy.start()
     barrier = pltpu.get_barrier_semaphore()
     for d in order:
@@ -70,6 +73,11 @@
 
     def col(t):
         return pl.ds(t * LANES, LANES)
+
+    for copy in inputs:
+        copy.wait()
+    reg = reg_ref[0]
+    step = step_ref[0]
 
     w2row = wo_ref[...]
     w2col = jnp.sum(jnp.where(lane[:, :hid] == sub[:, :hid], w2row, 0.0), axis=1, keepdims=True)
@@ -83,26 +91,33 @@
         q_ref[j] = jnp.zeros((hid, rows), F32)
 
     def pieces(src):
-        for t in range(tiles):
-            v = src[:, col(t)]
-            if t == tiles - 1:
-                v = jnp.where(lane < tail, v, 0.0)
-            for i, piece in enumerate(split3(v)):
+        for t in range(tiles - 1):
+            for i, piece in enumerate(split3(src[:, col(t)])):
                 g3_ref[i * hid:(i + 1) * hid, col(t)] = piece
+        for i, piece in enumerate(split3(src[:, main:dim])):
+            gt_ref[:, i * tail:(i + 1) * tail] = piece
 
     def forward(slot, c):
         rs = pl.ds(c * per, per)
-        prod = lax.dot_general(g3_ref[:, 0:main], xv[rs, 0:main], (((1,), (1,)), ((), ())), preferred_element_type=F32)
-        prod += lax.dot_general(g3_ref[:, main:width], xt[rs, :], (((1,), (1,)), ((), ())), preferred_element_type=F32)
-        q_ref[slot, :, rs] = prod[0:hid] + (prod[hid:2 * hid] + prod[2 * hid:3 * hid])
-
+        prod = jnp.dot(g3_ref[...], xr[0:main, rs], preferred_element_type=F32)
+        prod_t = jnp.dot(gt_ref[...], xt[:, rs], preferred_element_type=F32)
+        q_ref[slot, :, rs] = prod[0:hid] + (prod[hid:2 * hid] + (prod[2 * hid:3 * hid] + prod_t))
+
+    gt_ref[...] = jnp.zeros_like(gt_ref)
+    xt[3 * tail:, :] = jnp.zeros((LANES - 3 * tail, rows), BF16)
     pieces(theta)
     for c in range(CHUNKS):
         rs = pl.ds(c * per, per)
         copies[c].wait()
-        xt[rs, :] = jnp.zeros((per, LANES), BF16)
-        xt[rs, 0:tail] = xv[rs, main:dim]
+        for i in range(3):
+            xt[i * tail:(i + 1) * tail, rs] = xr[main:dim, rs]
         forward(0, c)
+
+    def by_rows():
+        for c in range(rows // LANES):
+            for t in range(tiles - 1):
+                xv[col(c), col(t)] = xr[col(t), col(c)].T
+            xv[col(c), main:width] = xt[:, col(c)].T
 
     def zcopy(par, c, d):
         return pltpu.make_async_remote_copy(
@@ -165,21 +180,18 @@
                     d3_ref[p * hid:(p + 1) * hid, col(i)] = piece
             rs = pl.ds(c * per, per)
             lhs = d3_ref[:, rs]
-            pm = jnp.dot(lhs, xv[rs, 0:main], preferred_element_type=F32)
-            pt = jnp.dot(lhs, xt[rs, :], preferred_element_type=F32)
+            prod = jnp.dot(lhs, xv[rs, :], preferred_element_type=F32)
             if c == 0:
-                acc_ref[:, 0:main] = pm
-                acc_ref[:, main:width] = pt
+                acc_ref[...] = prod
             else:
-                acc_ref[:, 0:main] += pm
-                acc_ref[:, main:width] += pt
+                acc_ref[...] += prod
         lacc[it] = loss
         gw2 = jnp.sum(gw2.reshape(hid, LANES), axis=1, keepdims=True)
         for t in range(tiles):
             total = acc_ref[0:hid, col(t)] + (acc_ref[hid:2 * hid, col(t)] + acc_ref[2 * hid:3 * hid, col(t)])
             total = total * (in_scale * out_scale / rows)
             if t == tiles - 1:
-                total = jnp.where(lane == tail, gw2 * (out_scale / rows), total)
+                total = jnp.where(lane < tail, total, jnp.where(lane == tail, gw2 * (out_scale / rows), 0.0))
             g_ref[:, col(t)] = total + reg * theta[:, col(t)]
         for c in range(CHUNKS):
             for d in order:
@@ -196,6 +208,7 @@
     zero = jnp.zeros((8, LANES), F32)
 
     logits(0, coefs_of(jnp.where(lane8 == 0, 1.0, zero), 1))
+    by_rows()
     gradient(0, 0)
     pieces(g_ref)
     for c in range(CHUNKS):
@@ -295,12 +308,19 @@
 
     lax.fori_loop(1, NUM_ITERS, body, 0)
 
-    wnew_ref[:, 0:main] = theta[:, 0:main]
-    wnew_ref[:, main:dim] = theta[:, main:dim]
+
+def unpack(rows, theta, lacc, wnew_ref, wonew_ref, loss_ref):
+    hid, dim = wnew_ref.shape
+    wnew_ref[...] = theta[:, 0:dim]
+    lane = lax.broadcasted_iota(jnp.int32, (hid, LANES), 1)
+    sub = lax.broadcasted_iota(jnp.int32, (hid, LANES), 0)
     w2col = theta[:, dim:dim + 1]
     wonew_ref[...] = jnp.sum(jnp.where(lane == sub, w2col, 0.0), axis=0, keepdims=True)[:, 0:hid]
+    row = jnp.zeros((1, LANES), F32)
     for k in range(NUM_ITERS):
-        loss_ref[k] = jnp.sum(lacc[k]) / rows
+        loss = jnp.sum(jnp.sum(lacc[k], axis=0, keepdims=True), axis=1, keepdims=True)
+        row = jnp.where(lane[0:1] == k, loss, row)
+    loss_ref[...] = row[:, 0:NUM_ITERS] / rows
 
 
 def solution(mesh):
@@ -312,26 +332,31 @@
         width = dim // LANES * LANES + LANES
         per = rows // CHUNKS
         vmem = pl.BlockSpec(memory_space=pltpu.VMEM)
-        smem = pl.BlockSpec(memory_space=pltpu.SMEM)
-        wnew, wonew, losses = pl.pallas_call(
+        hbm = pl.BlockSpec(memory_space=pltpu.HBM)
+        theta, lacc = pl.pallas_call(
             functools.partial(kernel, n, rows, hid, dim, hid * n),
             out_shape=(
-                jax.ShapeDtypeStruct((hid, dim), F32),
-                jax.ShapeDtypeStruct((1, hid), F32),
-                jax.ShapeDtypeStruct((NUM_ITERS,), F32),
+                jax.ShapeDtypeStruct((hid, width), F32),
+                jax.ShapeDtypeStruct((NUM_ITERS, 8, LANES), F32),
             ),
-            in_specs=[pl.BlockSpec(memory_space=pltpu.HBM), vmem, vmem, vmem, smem, smem],
-            out_specs=(vmem, vmem, smem),
+            in_specs=[hbm] * 6,
+            out_specs=(vmem, vmem),
             scratch_shapes=[
-                pltpu.VMEM((rows, dim), BF16),
-                pltpu.VMEM((rows, LANES), BF16),
+                pltpu.VMEM((rows, width), BF16),
+                pltpu.VMEM((dim, rows), BF16),
+                pltpu.VMEM((LANES, rows), BF16),
+                pltpu.VMEM((rows // LANES, LANES), F32),
+                pltpu.VMEM((hid, dim), F32),
+                pltpu.VMEM((1, hid), F32),
+                pltpu.SMEM((1,), F32),
+                pltpu.SMEM((1,), F32),
                 pltpu.VMEM((NUM_ITERS, hid, rows), F32),
                 pltpu.VMEM((hid, rows), F32),
                 pltpu.VMEM((hid, rows), F32),
                 pltpu.VMEM((3 * hid, rows), BF16),
-                pltpu.VMEM((3 * hid, width), BF16),
+                pltpu.VMEM((3 * hid, dim // LANES * LANES), BF16),
+                pltpu.VMEM((hid, LANES), BF16),
                 pltpu.VMEM((3 * hid, width), F32),
-                pltpu.VMEM((hid, width), F32),
                 pltpu.VMEM((hid, width), F32),
                 pltpu.VMEM((HIST, hid, width), F32),
                 pltpu.VMEM((HIST, hid, width), F32),
@@ -340,8 +365,8 @@
                 pltpu.VMEM((rows // LANES, LANES), F32),
                 pltpu.VMEM((n, 1, LANES), F32),
                 pltpu.VMEM((10, 8, LANES), F32),
-                pltpu.VMEM((NUM_ITERS, 8, LANES), F32),
                 pltpu.SemaphoreType.DMA((CHUNKS,)),
+                pltpu.SemaphoreType.DMA((5,)),
                 pltpu.SemaphoreType.DMA((CHUNKS, n)),
                 pltpu.SemaphoreType.DMA((2, CHUNKS, n)),
                 pltpu.SemaphoreType.DMA((n,)),
@@ -350,8 +375,18 @@
             compiler_params=pltpu.CompilerParams(
                 collective_id=0, has_side_effects=True, vmem_limit_bytes=56 * 1024 * 1024
             ),
-        )(x, t.reshape(rows // LANES, LANES), w, wo.reshape(1, hid), reg, step)
-        return wnew, wonew.reshape(hid), losses
+        )(x.T, t.reshape(rows // LANES, LANES), w, wo.reshape(1, hid), reg, step)
+        wnew, wonew, losses = pl.pallas_call(
+            functools.partial(unpack, rows),
+            out_shape=(
+                jax.ShapeDtypeStruct((hid, dim), F32),
+                jax.ShapeDtypeStruct((1, hid), F32),
+                jax.ShapeDtypeStruct((1, NUM_ITERS), F32),
+            ),
+            in_specs=[vmem, vmem],
+            out_specs=(vmem,) * 3,
+        )(theta, lacc)
+        return wnew, wonew.reshape(hid), losses.reshape(NUM_ITERS)
 
     specs_in = (P("prob", None), P("prob"), P(("prob", "feat"), None), P(("prob", "feat")), P("prob"), P("prob"))
     specs_out = (P(("prob", "feat"), None), P(("prob", "feat")), P("prob"))

time: 84.5 us -> 69.3 us (0.82)
  local copies, waits for them, and re-layouts: 14.3 us -> 0 us
    unnamed x4 -> x0, local copies, waits for them, and re-layouts: 14.3 us -> none
    pallas_call x1, Pallas kernels: 67.9 us -> 65.6 us  [local_solve(): pl.pallas_call(functools.partial(kernel, n, rows, hid, dim, hid * n), out...]
    pallas_call x0 -> x1, Pallas kernels: none -> 1.65 us  [local_solve(): pl.pallas_call(functools.partial(unpack, rows), out_shape=(jax.ShapeDtype...]
where the time goes in v2:
time: 69.3 us; the launch traced here: 69.2 us
  Pallas kernels  67.3 us (97%)
  between operations  1.93 us (3%)
    pallas_call x1, Pallas kernels, local_solve(): pl.pallas_call(functools.partial(kernel, n, rows, hid, dim, hid * n), out...  65.6 us
    pallas_call x1, Pallas kernels, local_solve(): pl.pallas_call(functools.partial(unpack, rows), out_shape=(jax.ShapeDtype...  1.65 us

profile of v2, /device:TPU:113, one launch (start us, length us, event | category | flops | bytes accessed | tf_op | source)
XLA Modules:
  0.0 69.2 jit_solution(16643041996808702163)
XLA Ops:
  1.9 65.6 %shard_map.85 = (f32[64,896]{1,0:T(8,128)}, f32[6,8,128]{2,1,0:T(8,128)}) custom-call(bf16[784,4096]{1,0:T(8,128)(2,1)} %bitcast.5, f32[32,128]{1,0:T(8,128)} %bitcast.6, f32[64,784]{1,0:T(8,128)} %w_hbm.1, f32[1,64]{1,0:T(1,128)} %bitcast.7, f32[1]{0:T(128)S(6)} %copy.9.reg_hbm, f32[1]{0:T(128)S(6)} %copy.10.step_hbm), custom_call_target="tpu_custom_call" | custom-call | tf_op jit(solution)/shard_map/pallas_call | solution.py:336
  67.6 1.7 %shard_map.86 = (f32[64,784]{1,0:T(8,128)}, f32[1,64]{1,0:T(1,128)}, f32[1,6]{1,0:T(1,128)}) custom-call(f32[64,896]{1,0:T(8,128)} %get-tuple-element.8.theta, f32[6,8,128]{2,1,0:T(8,128)} %get-tuple-element.9.lacc), custom_call_target="tpu_custom_call" | custom-call | tf_op jit(solution)/shard_map/pallas_call | solution.py:379

commit v3 on v2

v3 whole, which is shorter than its diff:
```python
import functools
import math

import jax
import jax.numpy as jnp
from jax import lax
from jax.experimental import pallas as pl
from jax.experimental.pallas import tpu as pltpu
from jax.sharding import PartitionSpec as P

NUM_ITERS = 6
HIST = 3
CHUNKS = 4
SPLIT = (1, 1, 2)
VMEM_BYTES = 50 * 1024 * 1024
LANES = 128
F32 = jnp.float32
BF16 = jnp.bfloat16
MESH = pl.DeviceIdType.MESH


def split3(v):
    hi = v.astype(BF16)
    rest = v - hi.astype(F32)
    mid = rest.astype(BF16)
    lo = (rest - mid.astype(F32)).astype(BF16)
    return hi, mid, lo


def kernel(
    n, rows, hid, dim, out_units,
    x_hbm, t_hbm, w_hbm, wo_hbm, reg_ref, step_ref,
    theta, lacc,
    xv, xr, xt, t_ref, w_ref, wo_ref, q_ref, h_ref, u_ref, d3_ref, g3_ref, gt_ref, acc_ref, tail_ref, g_ref,
    s_ref, y_ref, w2b_ref, zbuf, r_ref, dbuf,
    xsem, isem, zsend, zrecv, dsend, drecv,
):
    main = dim // LANES * LANES
    tail = dim - main
    width = main + LANES
    tiles = width // LANES
    groups = hid // 8
    per = rows // CHUNKS
    blocks = per // LANES
    sizes = [v * rows // (sum(SPLIT) * LANES) for v in SPLIT]
    spans = [(sum(sizes[:i]), sum(sizes[:i + 1])) for i in range(len(sizes))]
    in_scale = 1.0 / math.sqrt(dim)
    out_scale = 1.0 / math.sqrt(out_units)
    me = lax.axis_index("feat")

    def peer(d):
        return lax.rem(me + d, n)

    order = sorted(range(1, n), key=lambda d: -min(d, n - d))

    copies = [
        pltpu.make_async_copy(x_hbm.at[:, pl.ds(c * per, per)], xr.at[:, pl.ds(c * per, per)], xsem.at[c])
        for c in range(CHUNKS)
    ]
    inputs = [
        pltpu.make_async_copy(src, dst, isem.at[i])
        for i, (src, dst) in enumerate(
            ((w_hbm, w_ref), (wo_hbm, wo_ref), (t_hbm, t_ref)))
    ]
    for copy in inputs[:2] + copies + inputs[2:]:
        copy.start()
    barrier = pltpu.get_barrier_semaphore()
    for d in order:
        pl.semaphore_signal(barrier, inc=1, device_id={"feat": peer(d)}, device_id_type=MESH)

    lane8 = lax.broadcasted_iota(jnp.int32, (8, LANES), 1)
    lane = lax.broadcasted_iota(jnp.int32, (hid, LANES), 1)
    sub = lax.broadcasted_iota(jnp.int32, (hid, LANES), 0)

    def g8(v):
        return v.reshape(groups, 8, LANES)

    def col(t):
        return pl.ds(t * LANES, LANES)

    def pieces(src):
        for t in range(tiles - 1):
            for i, piece in enumerate(split3(src[:, col(t)])):
                g3_ref[i * hid:(i + 1) * hid, col(t)] = piece
        for i, piece in enumerate(split3(src[:, main:dim])):
            gt_ref[:, i * tail:(i + 1) * tail] = piece

    def forward(slot, rs):
        prod = jnp.dot(g3_ref[...], xr[0:main, rs], preferred_element_type=F32)
        prod_t = jnp.dot(gt_ref[...], xt[:, rs], preferred_element_type=F32)
        q_ref[slot, :, rs] = prod[0:hid] + (prod[hid:2 * hid] + (prod[2 * hid:3 * hid] + prod_t))

    def zcopy(par, c, d):
        return pltpu.make_async_remote_copy(
            src_ref=zbuf.at[par, me, pl.ds(spans[c][0], sizes[c])], dst_ref=zbuf.at[par, me, pl.ds(spans[c][0], sizes[c])],
            send_sem=zsend.at[c, d], recv_sem=zrecv.at[par, c, me],
            device_id={"feat": peer(d)}, device_id_type=MESH)

    def zarrive(par, c, d):
        source = peer(n - d)
        return pltpu.make_async_remote_copy(
            src_ref=zbuf.at[par, source, pl.ds(spans[c][0], sizes[c])],
            dst_ref=zbuf.at[par, source, pl.ds(spans[c][0], sizes[c])],
            send_sem=zsend.at[c, d], recv_sem=zrecv.at[par, c, source],
            device_id={"feat": source}, device_id_type=MESH)

    def dcopy(d):
        return pltpu.make_async_remote_copy(
            src_ref=dbuf.at[me], dst_ref=dbuf.at[me], send_sem=dsend.at[d], recv_sem=drecv.at[me],
            device_id={"feat": peer(d)}, device_id_type=MESH)

    def darrive(d):
        source = peer(n - d)
        return pltpu.make_async_remote_copy(
            src_ref=dbuf.at[source], dst_ref=dbuf.at[source], send_sem=dsend.at[d], recv_sem=drecv.at[source],
            device_id={"feat": source}, device_id_type=MESH)

    def logits(par, coefs, start, stop):
        scaled = [v * in_scale for v in coefs]
        for b in range(start, stop):
            cs = col(b)
            pre = scaled[0] * g8(q_ref[0, :, cs])
            for j in range(1, len(coefs)):
                pre += scaled[j] * g8(q_ref[j, :, cs])
            act = jnp.tanh(pre)
            h_ref[:, cs] = act.reshape(hid, LANES)
            part = jnp.sum(act * g8(w2b_ref[...]), axis=0)
            zbuf[par, me, b:b + 1, :] = jnp.sum(part, axis=0, keepdims=True) * out_scale
        for c, span in enumerate(spans):
            if start < span[1] <= stop:
                for d in order:
                    zcopy(par, c, d).start()

    def slopes():
        for b in range(rows // LANES):
            act = h_ref[:, col(b)]
            u_ref[:, col(b)] = w2b_ref[...] * (1.0 - act * act)

    def gradient(it, par, reg, use):
        loss = jnp.zeros((8, LANES), F32)
        gw2 = jnp.zeros((groups, 8, LANES), F32)
        for c, (start, stop) in enumerate(spans):
            for d in order:
                zarrive(par, c, d).wait_recv()
            z = zbuf[par, 0, start:stop, :]
            for i in range(1, n):
                z += zbuf[par, i, start:stop, :]
            t = t_ref[start:stop, :]
            cost = jnp.maximum(z, 0.0) + jnp.log1p(jnp.exp(-jnp.abs(z))) - t * z
            loss += jnp.sum(cost.reshape((stop - start) // 8, 8, LANES), axis=0)
            r_ref[start:stop, :] = jax.nn.sigmoid(z) - t
            for i in range(start, stop):
                rrow = r_ref[i:i + 1, :]
                gw2 += g8(h_ref[:, col(i)] * rrow)
                for p, piece in enumerate(split3(u_ref[:, col(i)] * rrow)):
                    d3_ref[p * hid:(p + 1) * hid, col(i)] = piece
            rs = pl.ds(start * LANES, (stop - start) * LANES)
            prod_t = lax.dot_general(
                xr[main:dim, rs], d3_ref[:, rs], (((1,), (1,)), ((), ())), preferred_element_type=F32)
            last = prod_t if c == 0 else last + prod_t
            if c < len(spans) - 1:
                prod = jnp.dot(d3_ref[:, rs], xv[rs, :], preferred_element_type=F32)
                if c == 0:
                    acc_ref[...] = prod
                else:
                    acc_ref[...] += prod
        lacc[it] = loss
        gw2 = jnp.sum(gw2.reshape(hid, LANES), axis=1, keepdims=True)
        rs = pl.ds(spans[-1][0] * LANES, sizes[-1] * LANES)
        def finish(t, total):
            g_ref[par, :, col(t)] = (g8(total) + reg * g8(theta[:, col(t)])).reshape(hid, LANES)
            use(t)

        scale = in_scale * out_scale / rows
        for start in range(0, main, 2 * LANES):
            cs = slice(start, start + 2 * LANES)
            prod = jnp.dot(d3_ref[:, rs], xv[rs, cs], preferred_element_type=F32) + acc_ref[:, cs]
            prod = (prod[0:hid] + (prod[hid:2 * hid] + prod[2 * hid:3 * hid])) * scale
            finish(start // LANES, prod[:, :LANES])
            finish(start // LANES + 1, prod[:, LANES:])
            if start == 0:
                last = last[:, 0:hid] + (last[:, hid:2 * hid] + last[:, 2 * hid:3 * hid])
                tail_ref[:, 0:tail] = last.T * scale
                finish(tiles - 1, jnp.where(lane == tail, gw2 * (out_scale / rows), tail_ref[...]))

    def sent(par):
        for c in range(len(spans)):
            for d in order:
                zcopy(par, c, d).wait_send()

    def by_rows():
        def rows_of(c, carry):
            cs = pl.ds(pl.multiple_of(c * 2 * LANES, 2 * LANES), 2 * LANES)
            for t in range(tiles - 1):
                xv[cs, col(t)] = xr[col(t), cs].T
            return carry

        lax.fori_loop(0, rows // (2 * LANES), rows_of, 0)

    gt_ref[...] = jnp.zeros_like(gt_ref)
    tail_ref[...] = jnp.zeros_like(tail_ref)
    xt[3 * tail:, :] = jnp.zeros((LANES - 3 * tail, rows), BF16)
    for copy in inputs[:2]:
        copy.wait()
    w2col = jnp.sum(jnp.where(lane[:, :hid] == sub[:, :hid], wo_ref[...], 0.0), axis=1, keepdims=True)
    theta[:, main:width] = jnp.where(lane == tail, w2col, 0.0)
    theta[:, 0:main] = w_ref[:, 0:main]
    theta[:, main:dim] = w_ref[:, main:dim]
    w2b_ref[...] = jnp.broadcast_to(w2col, (hid, LANES))
    pieces(theta)
    pl.semaphore_wait(barrier, n - 1)

    one = jnp.ones((8, LANES), F32)
    for c in range(CHUNKS):
        rs = pl.ds(c * per, per)
        copies[c].wait()
        for i in range(3):
            xt[i * tail:(i + 1) * tail, rs] = xr[main:dim, rs]
        forward(0, rs)
        logits(0, [one], c * blocks, (c + 1) * blocks)
    for copy in inputs[2:]:
        copy.wait()
    reg = jnp.full((8, LANES), reg_ref[0], F32)
    step = jnp.full((8, LANES), step_ref[0], F32)
    slopes()
    by_rows()

    def first(t):
        s = -step * g8(g_ref[0, :, col(t)])
        s_ref[0, :, col(t)] = s.reshape(hid, LANES)
        theta[:, col(t)] = (g8(theta[:, col(t)]) + s).reshape(hid, LANES)

    gradient(0, 0, reg, first)
    pieces(g_ref.at[0])
    coefs = [one, -step]
    sigma = {0: [-step]}
    w2b_ref[...] = jnp.broadcast_to(theta[:, dim:dim + 1], (hid, LANES))
    for c in range(CHUNKS):
        rs = pl.ds(c * per, per)
        forward(1, rs)
        logits(1, coefs, c * blocks, (c + 1) * blocks)
    sent(0)

    rho, sy, yy, sg, yg = {}, {}, {}, {}, {}
    update = None
    for k in range(1, NUM_ITERS):
        par = k % 2
        if k > 1:
            w2b_ref[...] = jnp.broadcast_to(theta[:, dim:dim + 1], (hid, LANES))
            for start, stop in spans:
                logits(par, coefs, start, stop)
            for t in range(tiles - 1):
                update(t)
        slopes()
        new = k - 1
        pairs = list(range(max(0, k - HIST), k))
        dots = [jnp.zeros((8, LANES), F32)] * (2 + 2 * len(pairs))

        def products(t):
            g = g8(g_ref[par, :, col(t)])
            y = g - g8(g_ref[1 - par, :, col(t)])
            y_ref[new % HIST, :, col(t)] = y.reshape(hid, LANES)
            ss = [g8(s_ref[i % HIST, :, col(t)]) for i in pairs]
            ys = [g8(y_ref[i % HIST, :, col(t)]) for i in pairs[:-1]] + [y]
            terms = [(ss[-1], g), (y, g)] + [(v, y) for v in ss] + [(v, y) for v in ys]
            dots[:] = [d + jnp.sum(a * b, axis=0) for d, (a, b) in zip(dots, terms)]

        gradient(k, par, reg, products)
        row = jnp.zeros((1, LANES), F32)
        for i, d in enumerate(dots):
            d = jnp.sum(jnp.sum(d, axis=0, keepdims=True), axis=1, keepdims=True)
            row = jnp.where(lane8[0:1] == i, d, row)
        dbuf[me] = row
        for d in order:
            dcopy(d).start()
        if k < NUM_ITERS - 1:
            pieces(g_ref.at[par])

            def multiply(c, carry):
                forward(k + 1, pl.ds(pl.multiple_of(c * per, per), per))
                return carry

            lax.fori_loop(0, CHUNKS, multiply, 0)
        sent(par)
        for d in order:
            darrive(d).wait_recv()
        total = dbuf[0]
        for i in range(1, n):
            total += dbuf[i]
        vals = [jnp.broadcast_to(total[:, i:i + 1], (8, LANES)) for i in range(len(dots))]
        for i, v in zip(pairs, vals[2:2 + len(pairs)]):
            sy[i, new] = v
        for i, v in zip(pairs, vals[2 + len(pairs):]):
            yy[i, new] = yy[new, i] = v
        for i in pairs[:-1]:
            sg[i] = sg[i] + sy[i, new]
            yg[i] = yg[i] + yy[i, new]
        sg[new], yg[new] = vals[0], vals[1]
        rho[new] = 1.0 / sy[new, new]
        gamma = sy[new, new] / yy[new, new]
        a, diff = {}, {}
        for i in reversed(pairs):
            v = sg[i]
            for j in range(i + 1, k):
                v = v - a[j] * sy[i, j]
            a[i] = rho[i] * v
        for i in pairs:
            v = yg[i]
            for j in reversed(pairs):
                v = v - a[j] * yy[i, j]
            v = gamma * v
            for j in pairs:
                if j < i:
                    v = v + diff[j] * sy[j, i]
            diff[i] = a[i] - rho[i] * v
        cg = -step * gamma
        cy = {i: -cg * a[i] for i in pairs}
        cs = {i: -step * diff[i] for i in pairs}

        def update(t, k=k, par=par, pairs=pairs, cg=cg, cy=cy, cs=cs):
            s = cg * g8(g_ref[par, :, col(t)])
            for i in pairs:
                s = s + cy[i] * g8(y_ref[i % HIST, :, col(t)])
                s = s + cs[i] * g8(s_ref[i % HIST, :, col(t)])
            s_ref[k % HIST, :, col(t)] = s.reshape(hid, LANES)
            theta[:, col(t)] = (g8(theta[:, col(t)]) + s).reshape(hid, LANES)

        update(tiles - 1)
        part = [None] * (k + 1)

        def plus(j, v):
            part[j] = v if part[j] is None else part[j] + v

        plus(k, cg)
        for i in pairs:
            plus(i + 1, cy[i])
            plus(i, -cy[i])
            for j, v in enumerate(sigma[i]):
                plus(j, cs[i] * v)
        sigma[k] = [jnp.zeros((8, LANES), F32) if v is None else v for v in part]
        coefs = [coefs[0]] + [
            (coefs[j + 1] if j + 1 < len(coefs) else 0.0) + sigma[k][j] for j in range(k + 1)
        ]
        for d in order:
            dcopy(d).wait_send()

    for t in range(tiles - 1):
        update(t)


def unpack(rows, theta, lacc, wnew_ref, wonew_ref, loss_ref):
    hid, dim = wnew_ref.shape
    wnew_ref[...] = theta[:, 0:dim]
    lane = lax.broadcasted_iota(jnp.int32, (hid, LANES), 1)
    sub = lax.broadcasted_iota(jnp.int32, (hid, LANES), 0)
    w2col = theta[:, dim:dim + 1]
    wonew_ref[...] = jnp.sum(jnp.where(lane == sub, w2col, 0.0), axis=0, keepdims=True)[:, 0:hid]
    row = jnp.zeros((1, LANES), F32)
    for k in range(NUM_ITERS):
        loss = jnp.sum(jnp.sum(lacc[k], axis=0, keepdims=True), axis=1, keepdims=True)
        row = jnp.where(lane[0:1] == k, loss, row)
    loss_ref[...] = row[:, 0:NUM_ITERS] / rows


def solution(mesh):
    n = mesh.shape["feat"]

    def local_solve(x, t, w, wo, reg, step):
        rows, dim = x.shape
        hid = w.shape[0]
        width = dim // LANES * LANES + LANES
        vmem = pl.BlockSpec(memory_space=pltpu.VMEM)
        big = (x.T, t.reshape(rows // LANES, LANES), w, wo.reshape(1, hid))
        hbm = pl.BlockSpec(memory_space=pltpu.HBM)
        smem = pl.BlockSpec(memory_space=pltpu.SMEM)
        theta, lacc = pl.pallas_call(
            functools.partial(kernel, n, rows, hid, dim, hid * n),
            out_shape=(
                jax.ShapeDtypeStruct((hid, width), F32),
                jax.ShapeDtypeStruct((NUM_ITERS, 8, LANES), F32),
            ),
            in_specs=[hbm] * 4 + [smem] * 2,
            out_specs=(vmem, vmem),
            scratch_shapes=[
                pltpu.VMEM((rows, dim // LANES * LANES), BF16),
                pltpu.VMEM((dim, rows), BF16),
                pltpu.VMEM((LANES, rows), BF16),
                pltpu.VMEM((rows // LANES, LANES), F32),
                pltpu.VMEM((hid, dim), F32),
                pltpu.VMEM((1, hid), F32),
                pltpu.VMEM((NUM_ITERS, hid, rows), F32),
                pltpu.VMEM((hid, rows), F32),
                pltpu.VMEM((hid, rows), F32),
                pltpu.VMEM((3 * hid, rows), BF16),
                pltpu.VMEM((3 * hid, dim // LANES * LANES), BF16),
                pltpu.VMEM((hid, LANES), BF16),
                pltpu.VMEM((3 * hid, dim // LANES * LANES), F32),
                pltpu.VMEM((hid, LANES), F32),
                pltpu.VMEM((2, hid, width), F32),
                pltpu.VMEM((HIST, hid, width), F32),
                pltpu.VMEM((HIST, hid, width), F32),
                pltpu.VMEM((hid, LANES), F32),
                pltpu.VMEM((2, n, rows // LANES, LANES), F32),
                pltpu.VMEM((rows // LANES, LANES), F32),
                pltpu.VMEM((n, 1, LANES), F32),
                pltpu.SemaphoreType.DMA((CHUNKS,)),
                pltpu.SemaphoreType.DMA((3,)),
                pltpu.SemaphoreType.DMA((len(SPLIT), n)),
                pltpu.SemaphoreType.DMA((2, len(SPLIT), n)),
                pltpu.SemaphoreType.DMA((n,)),
                pltpu.SemaphoreType.DMA((n,)),
            ],
            compiler_params=pltpu.CompilerParams(
                collective_id=0, has_side_effects=True, vmem_limit_bytes=VMEM_BYTES
            ),
        )(*(pltpu.with_memory_space_constraint(v, pltpu.HBM) for v in big), reg, step)
        wnew, wonew, losses = pl.pallas_call(
            functools.partial(unpack, rows),
            out_shape=(
                jax.ShapeDtypeStruct((hid, dim), F32),
                jax.ShapeDtypeStruct((1, hid), F32),
                jax.ShapeDtypeStruct((1, NUM_ITERS), F32),
            ),
            in_specs=[vmem, vmem],
            out_specs=(vmem,) * 3,
            compiler_params=pltpu.CompilerParams(vmem_limit_bytes=4 * 1024 * 1024),
        )(theta, lacc)
        return wnew, wonew.reshape(hid), losses.reshape(NUM_ITERS)

    specs_in = (P("prob", None), P("prob"), P(("prob", "feat"), None), P(("prob", "feat")), P("prob"), P("prob"))
    specs_out = (P(("prob", "feat"), None), P(("prob", "feat")), P("prob"))
    return jax.shard_map(local_solve, mesh=mesh, in_specs=specs_in, out_specs=specs_out, check_vma=False)
```

time: 69.3 us -> 63.3 us (0.913)
  Pallas kernels: 67.3 us -> 61.3 us
    pallas_call x1, Pallas kernels: 65.6 us -> 60.6 us  [local_solve(): pl.pallas_call(functools.partial(kernel, n, rows, hid, dim, hid * n), out...]
    pallas_call x1, Pallas kernels: 1.65 us -> 0.71 us  [local_solve(): pl.pallas_call(functools.partial(unpack, rows), out_shape=(jax.ShapeDtype...]
where the time goes in v3:
time: 63.3 us; the launch traced here: 63.2 us
  Pallas kernels  61.3 us (97%)
  between operations  1.93 us (3%)
    pallas_call x1, Pallas kernels, local_solve(): pl.pallas_call(functools.partial(kernel, n, rows, hid, dim, hid * n), out...  60.6 us

profile of v3, /device:TPU:113, one launch (start us, length us, event | category | flops | bytes accessed | tf_op | source)
XLA Modules:
  0.0 63.2 jit_solution(64771558634187128)
XLA Ops:
  1.9 60.6 %shard_map.85 = (f32[64,896]{1,0:T(8,128)S(1)}, f32[6,8,128]{2,1,0:T(8,128)S(1)}) custom-call(bf16[784,4096]{1,0:T(8,128)(2,1)} %bitcast.5, f32[32,128]{1,0:T(8,128)} %bitcast.6, f32[64,784]{1,0:T(8,128)} %w_hbm.1, f32[1,64]{1,0:T(1,128)} %bitcast.7, f32[1]{0:T(128)S(6)} %copy.9.reg_ref, f32[1]{0:T(128)S(6)} %copy.10.step_ref), custom_call_target="tpu_custom_call" | custom-call | tf_op jit(solution)/shard_map/pallas_call | solution.py:376
  62.5 0.7 %shard_map.86 = (f32[64,784]{1,0:T(8,128)}, f32[1,64]{1,0:T(1,128)}, f32[1,6]{1,0:T(1,128)}) custom-call(f32[64,896]{1,0:T(8,128)S(1)} %get-tuple-element.8.theta, f32[6,8,128]{2,1,0:T(8,128)S(1)} %get-tuple-element.9.lacc), custom_call_target="tpu_custom_call" | custom-call | tf_op jit(solution)/shard_map/pallas_call | solution.py:417

commit v4 on v3

--- a/solution.py
+++ b/solution.py
@@ -136,6 +136,10 @@
             act = h_ref[:, col(b)]
             u_ref[:, col(b)] = w2b_ref[...] * (1.0 - act * act)
 
+    def last_columns(rs):
+        return lax.dot_general(
+            xr[main:dim, rs], d3_ref[:, rs], (((1,), (1,)), ((), ())), preferred_element_type=F32)
+
     def gradient(it, par, reg, use):
         loss = jnp.zeros((8, LANES), F32)
         gw2 = jnp.zeros((groups, 8, LANES), F32)
@@ -155,15 +159,10 @@
                 for p, piece in enumerate(split3(u_ref[:, col(i)] * rrow)):
                     d3_ref[p * hid:(p + 1) * hid, col(i)] = piece
             rs = pl.ds(start * LANES, (stop - start) * LANES)
-            prod_t = lax.dot_general(
-                xr[main:dim, rs], d3_ref[:, rs], (((1,), (1,)), ((), ())), preferred_element_type=F32)
-            last = prod_t if c == 0 else last + prod_t
             if c < len(spans) - 1:
                 prod = jnp.dot(d3_ref[:, rs], xv[rs, :], preferred_element_type=F32)
-                if c == 0:
-                    acc_ref[...] = prod
-                else:
-                    acc_ref[...] += prod
+                sums = prod if c == 0 else sums + prod
+                last = last_columns(rs) if c == 0 else last + last_columns(rs)
         lacc[it] = loss
         gw2 = jnp.sum(gw2.reshape(hid, LANES), axis=1, keepdims=True)
         rs = pl.ds(spans[-1][0] * LANES, sizes[-1] * LANES)
@@ -174,11 +173,12 @@
         scale = in_scale * out_scale / rows
         for start in range(0, main, 2 * LANES):
             cs = slice(start, start + 2 * LANES)
-            prod = jnp.dot(d3_ref[:, rs], xv[rs, cs], preferred_element_type=F32) + acc_ref[:, cs]
+            prod = sums[:, cs] + jnp.dot(d3_ref[:, rs], xv[rs, cs], preferred_element_type=F32)
             prod = (prod[0:hid] + (prod[hid:2 * hid] + prod[2 * hid:3 * hid])) * scale
             finish(start // LANES, prod[:, :LANES])
             finish(start // LANES + 1, prod[:, LANES:])
             if start == 0:
+                last = last + last_columns(rs)
                 last = last[:, 0:hid] + (last[:, hid:2 * hid] + last[:, 2 * hid:3 * hid])
                 tail_ref[:, 0:tail] = last.T * scale
                 finish(tiles - 1, jnp.where(lane == tail, gw2 * (out_scale / rows), tail_ref[...]))
@@ -249,6 +249,8 @@
             w2b_ref[...] = jnp.broadcast_to(theta[:, dim:dim + 1], (hid, LANES))
             for start, stop in spans:
                 logits(par, coefs, start, stop)
+            for d in order:
+                dcopy(d).wait_send()
             for t in range(tiles - 1):
                 update(t)
         slopes()
@@ -317,11 +319,15 @@
         cy = {i: -cg * a[i] for i in pairs}
         cs = {i: -step * diff[i] for i in pairs}
 
-        def update(t, k=k, par=par, pairs=pairs, cg=cg, cy=cy, cs=cs):
+        def total_step(t, par=par, pairs=pairs, cg=cg, cy=cy, cs=cs):
             s = cg * g8(g_ref[par, :, col(t)])
             for i in pairs:
                 s = s + cy[i] * g8(y_ref[i % HIST, :, col(t)])
                 s = s + cs[i] * g8(s_ref[i % HIST, :, col(t)])
+            return s
+
+        def update(t, k=k, total_step=total_step):
+            s = total_step(t)
             s_ref[k % HIST, :, col(t)] = s.reshape(hid, LANES)
             theta[:, col(t)] = (g8(theta[:, col(t)]) + s).reshape(hid, LANES)
 
@@ -341,11 +347,12 @@
         coefs = [coefs[0]] + [
             (coefs[j + 1] if j + 1 < len(coefs) else 0.0) + sigma[k][j] for j in range(k + 1)
         ]
-        for d in order:
-            dcopy(d).wait_send()
 
     for t in range(tiles - 1):
-        update(t)
+        s = total_step(t)
+        theta[:, col(t)] = (g8(theta[:, col(t)]) + s).reshape(hid, LANES)
+    for d in order:
+        dcopy(d).wait_send()
 
 
 def unpack(rows, theta, lacc, wnew_ref, wonew_ref, loss_ref):

time: 63.3 us -> 62.7 us (level)
  no operation moved by 1% of the time
where the time goes in v4:
time: 62.7 us; the launch traced here: 62.6 us
  Pallas kernels  60.7 us (97%)
  between operations  1.93 us (3%)
    pallas_call x1, Pallas kernels, local_solve(): pl.pallas_call(functools.partial(kernel, n, rows, hid, dim, hid * n), out...  59.9 us

profile of v4, /device:TPU:113, one launch (start us, length us, event | category | flops | bytes accessed | tf_op | source)
XLA Modules:
  0.0 62.6 jit_solution(699735754714561336)
XLA Ops:
  1.9 59.9 %shard_map.85 = (f32[64,896]{1,0:T(8,128)S(1)}, f32[6,8,128]{2,1,0:T(8,128)S(1)}) custom-call(bf16[784,4096]{1,0:T(8,128)(2,1)} %bitcast.5, f32[32,128]{1,0:T(8,128)} %bitcast.6, f32[64,784]{1,0:T(8,128)} %w_hbm.1, f32[1,64]{1,0:T(1,128)} %bitcast.7, f32[1]{0:T(128)S(6)} %copy.9.reg_ref, f32[1]{0:T(128)S(6)} %copy.10.step_ref), custom_call_target="tpu_custom_call" | custom-call | tf_op jit(solution)/shard_map/pallas_call | solution.py:383
  61.9 0.7 %shard_map.86 = (f32[64,784]{1,0:T(8,128)}, f32[1,64]{1,0:T(1,128)}, f32[1,6]{1,0:T(1,128)}) custom-call(f32[64,896]{1,0:T(8,128)S(1)} %get-tuple-element.8.theta, f32[6,8,128]{2,1,0:T(8,128)S(1)} %get-tuple-element.9.lacc), custom_call_target="tpu_custom_call" | custom-call | tf_op jit(solution)/shard_map/pallas_call | solution.py:424
